TPU v7x, 128 devices: a whole 4x4x4 slice. The times are simulated.
128 devices in a mesh: psg: 16 (over x_hi, y, core), qry: 8 (over z, x_lo).
Axes of the slice: x: 4 (x_hi: 2, x_lo: 2; x = x_hi * 2 + x_lo), y: 4, z: 4, core: 2. Of those that a mesh axis runs over, the one named last changes fastest.
Arguments:
- hidden: bfloat16 [1024, 4096], P('qry'), may hold values from -6 to 6
- norm_gain: float32 [4096], replicated, may hold values from 0.5 to 1.5
- proj_weight: bfloat16 [4096, 4096], P('psg', 'qry'), may hold values from -0.09375 to 0.09375
- pq_codes: int32 [32768, 512], P('psg', 'qry'), may hold values from 0 to 255
- codebook: bfloat16 [512, 8, 256], P('qry'), may hold values from -560 to 560
- positives: int32 [1024], replicated, may hold values from 0 to 32767
Outputs:
- losses: float32 [1024], P('qry')
- hidden_grad: bfloat16 [1024, 4096], P('qry')
- weight_grad: float32 [4096, 4096], P('psg', 'qry')
- codebook_grad: float32 [512, 8, 256], P('qry')
All inputs are finite; a program needn't handle non-finite values.
Results may differ from a plain program's by a relative error of at most 0.019.
The roundings to bfloat16 on the way count: a program that leaves them out, or rounds other values in their place, can miss the bound.
Values may be sent and summed in bfloat16 or wider, within the bound.
A program may use at most 128 MiB of HBM per device.

v0:
```python
import jax
import jax.numpy as jnp
from jax import lax
from jax.sharding import Mesh
from jax.sharding import PartitionSpec as P

QRY = ("qry_0", "qry_1")
score_scale = 0.0625
norm_eps = 1e-06


def summed_rows(x, axes, dim):
    if not axes:
        return x
    nearer = lax.psum_scatter(x, axes[0], scatter_dimension=dim, tiled=True)
    return summed_rows(nearer, axes[1:], dim)


def sent_to_all(x, axis):
    copies = jnp.broadcast_to(x, (lax.axis_size(axis), *x.shape))
    return lax.all_to_all(copies, axis, split_axis=0, concat_axis=0, tiled=True)


def gathered_once(x, axis):
    leaves = jax.tree.leaves(x)
    turns = sorted(range(len(leaves)), key=lambda k: -leaves[k].size)
    width = (1, *leaves[turns[0]].shape)[-1]
    lines = [
        jnp.pad(leaves[k].reshape(-1), (0, -leaves[k].size % width)).reshape(-1, width)
        for k in turns
    ]
    both, at, found = (sent_to_all(jnp.concatenate(lines), axis), 0, {})
    for k, line in zip(turns, lines):
        piece = both[:, at : at + len(line)].reshape(len(both), -1)
        found[k] = piece[:, : leaves[k].size].reshape(-1, *leaves[k].shape)
        at += len(line)
    numbers = iter(range(len(leaves)))
    return jax.tree.map(lambda _: found[next(numbers)], x)


def folded_in_pairs(pieces, combine):
    while len(jax.tree.leaves(pieces)[0]) > 1:
        pieces = jax.vmap(combine)(
            *(jax.tree.map(lambda part: part[side::2], pieces) for side in (0, 1))
        )
    return jax.tree.map(lambda part: part[0], pieces)


def joined_all(x, axis, combine):
    pieces = gathered_once(x, axis)
    return folded_in_pairs(pieces, combine)


def code_hot(code_block, book):
    levels = lax.broadcasted_iota(jnp.int32, code_block.shape + (book.shape[2],), 2)
    return (code_block[:, :, None] == levels).astype(jnp.bfloat16)


def per_device(hidden, norm_gain, proj_weight, pq_codes, codebook, positives):
    gathered = lax.all_gather(hidden, QRY, axis=0, tiled=True)
    floats_all = gathered.astype(jnp.float32)
    inverse_all = lax.rsqrt(jnp.mean(floats_all * floats_all, axis=1, keepdims=True) + norm_eps)
    normed = (floats_all * inverse_all * norm_gain[None, :]).astype(jnp.bfloat16)
    columns = proj_weight.shape[1]
    whole_weight = lax.all_gather(proj_weight, "psg", axis=0, tiled=True)
    query_float = jnp.dot(normed, whole_weight, preferred_element_type=jnp.float32)
    queries = query_float.astype(jnp.bfloat16)
    passage_count = pq_codes.shape[0]
    sub_count = codebook.shape[0]
    sub_width = codebook.shape[1]
    block_rows = min(passage_count, 512)
    code_blocks = pq_codes.reshape(passage_count // block_rows, block_rows, sub_count)

    def decode(code_block):
        hot_table = code_hot(code_block, codebook)
        vectors = jnp.einsum(
            "pmk,mdk->pmd", hot_table, codebook, preferred_element_type=jnp.float32
        )
        return vectors.astype(jnp.bfloat16).reshape(block_rows, columns)

    passages = lax.map(decode, code_blocks).reshape(passage_count, columns)
    partial_value = (
        lax.dot_general(
            queries, passages, (((1,), (1,)), ((), ())), preferred_element_type=jnp.float32
        )
        * score_scale
    )
    qry_index = lax.axis_index(QRY)
    own_rows = hidden.shape[0]
    scores = summed_rows(partial_value, QRY, 0)
    row_targets = lax.dynamic_slice_in_dim(positives, qry_index * own_rows, own_rows, 0)
    local_target = row_targets - lax.axis_index("psg") * passage_count
    target = lax.broadcasted_iota(jnp.int32, scores.shape, 1) == local_target[:, None]
    local_max = jnp.max(scores, axis=1)
    positive_part = jnp.sum(jnp.where(target, scores, 0.0), axis=1)
    local_total = jnp.sum(jnp.exp(scores - local_max[:, None]), axis=1)

    def combine(first, second):
        higher = jnp.maximum(first[0], second[0])
        joined = first[1] * jnp.exp(first[0] - higher) + second[1] * jnp.exp(second[0] - higher)
        return (higher, joined, first[2] + second[2])

    row_max, row_total, positive_score = joined_all(
        (local_max, local_total, positive_part), "psg", combine
    )
    losses = jnp.log(row_total) + row_max - positive_score
    score_grad = (
        jnp.exp(scores - row_max[:, None]) / row_total[:, None] - target.astype(jnp.float32)
    ).astype(jnp.bfloat16)
    all_grad = lax.all_gather(score_grad, QRY, axis=0, tiled=True)
    query_part = jnp.dot(all_grad, passages, preferred_element_type=jnp.float32) * score_scale
    query_grad = lax.psum(query_part, "psg").astype(jnp.bfloat16)
    passage_grad = (
        lax.dot_general(
            all_grad, queries, (((0,), (0,)), ((), ())), preferred_element_type=jnp.float32
        )
        * score_scale
    ).astype(jnp.bfloat16)
    grad_blocks = passage_grad.reshape(
        passage_count // block_rows, block_rows, sub_count, sub_width
    )

    def add_book(carry, paired):
        code_block, grad_block = paired
        hot_table = code_hot(code_block, codebook)
        return (
            carry
            + jnp.einsum("pmk,pmd->mdk", hot_table, grad_block, preferred_element_type=jnp.float32),
            None,
        )

    book_part, unused = lax.scan(
        add_book, jnp.zeros(codebook.shape, jnp.float32), (code_blocks, grad_blocks)
    )
    codebook_grad = lax.psum(book_part.astype(jnp.bfloat16), "psg").astype(jnp.float32)
    row_span = proj_weight.shape[0]
    normed_rows = lax.dynamic_slice_in_dim(normed, lax.axis_index("psg") * row_span, row_span, 1)
    weight_grad = lax.dot_general(
        normed_rows, query_grad, (((0,), (0,)), ((), ())), preferred_element_type=jnp.float32
    )
    norm_part = lax.dot_general(
        query_grad, whole_weight, (((1,), (1,)), ((), ())), preferred_element_type=jnp.float32
    )
    norm_back = lax.psum_scatter(
        norm_part.astype(jnp.bfloat16), QRY, scatter_dimension=0, tiled=True
    ).astype(jnp.float32)
    floats_own = hidden.astype(jnp.float32)
    inverse_own = lax.rsqrt(jnp.mean(floats_own * floats_own, axis=1, keepdims=True) + norm_eps)
    scaled = norm_back * norm_gain[None, :]
    hidden_grad = (
        inverse_own * scaled
        - floats_own
        * inverse_own
        * inverse_own
        * inverse_own
        * jnp.mean(scaled * floats_own, axis=1, keepdims=True)
    ).astype(jnp.bfloat16)
    return (losses, hidden_grad, weight_grad, codebook_grad)


def solution(mesh):
    split = Mesh(mesh.devices.reshape(mesh.shape["psg"], 4, 2), ("psg", "qry_0", "qry_1"))
    return jax.shard_map(
        per_device,
        mesh=split,
        in_specs=(P(QRY, None), P(), P("psg", QRY), P("psg", QRY), P(QRY, None, None), P()),
        out_specs=(P(QRY), P(QRY, None), P("psg", QRY), P(QRY, None, None)),
        check_vma=False,
    )
```

profile of v0, /device:TPU:1, one launch (start us, length us, event | category | flops | bytes accessed | tf_op | source)
XLA Modules:
  0.0 852.5 jit_solution(15345686447529952865)
XLA Ops:
  7.2 0.7 all-gather.4.cloned.1.call-update
  7.9 0.7 all-gather.6.cloned.1.call-update
  8.7 1.1 copy.27
  9.8 33.1 %while.21 = (s32[]{:T(128)}, bf16[4,512,512]{2,1,0:T(8,128)(2,1)}, s32[4,512,64]{1,2,0:T(8,128)S(1)}, bf16[64,8,256]{2,1,0:T(8,128)(2,1)}, s32[]{:T(128)}) while((s32[]{:T(128)}, bf16[4,512,512]{2,1,0:T(8,128)(2,1)}, s32[4,512,64]{1,2,0:T(8,128)S(1)}, bf16[64,8,256]{2,1,0:T(8,128)(2,1)}, s32[]{:T(128)}) %tuple.74), condition=%wide.region_2.3_spmd, body=%wide.region_1.2_spmd.sunk | while | flops 142868480 | bytes 3277377 | solution.py:81
  9.8 7.2 fusion.43
  17.0 0.2 copy.29
  17.2 0.8 constant_dynamic-update-slice_fusion.2
  18.1 7.2 fusion.43
  25.5 0.9 constant_dynamic-update-slice_fusion.2
  26.4 7.2 fusion.43
  33.8 0.8 constant_dynamic-update-slice_fusion.2
  34.6 7.2 fusion.43
  42.0 0.9 constant_dynamic-update-slice_fusion.2
  42.9 138.0 %all-gather.4.cloned.1.call-done = bf16[1024,4096]{1,0:T(8,128)(2,1)} async-done(((bf16[128,4096]{1,0:T(8,128)(2,1)}), bf16[1024,4096]{1,0:T(8,128)(2,1)}) %all-gather.4.cloned.1.call-update) | async-done | bytes 8388624 | tf_op jit(solution)/shard_map/all_gather | solution.py:60
  180.9 5.1 fusion.10
  186.0 10.3 %fusion.12 = bf16[1024,4096]{1,0:T(8,128)(2,1)} fusion(bf16[1024,4096]{1,0:T(8,128)(2,1)} %all-gather.4.cloned.1.call-done, f32[4096]{0:T(1024)S(1)} %copy-done.1, f32[1024]{0:T(1024)S(1)} %add_rsqrt_fusion), kind=kLoop, calls=%fused_computation.19 | loop fusion | flops 16777216 | bytes 16797696 | tf_op jit(solution)/shard_map/convert_element_type | solution.py:63
  196.3 43.5 %all-gather.6.cloned.1.call-done = bf16[4096,512]{1,0:T(8,128)(2,1)} async-done(((bf16[256,512]{1,0:T(8,128)(2,1)}), bf16[4096,512]{1,0:T(8,128)(2,1)}) %all-gather.6.cloned.1.call-update) | async-done | bytes 4194320 | tf_op jit(solution)/shard_map/all_gather | solution.py:65
  239.8 9.1 %convolution_convert_fusion.1 = bf16[1024,512]{1,0:T(8,128)(2,1)S(1)} fusion(bf16[1024,4096]{1,0:T(8,128)(2,1)} %fusion.12, bf16[4096,512]{1,0:T(8,128)(2,1)} %all-gather.6.cloned.1.call-done), kind=kOutput, calls=%fused_computation.35 | convolution fusion | flops 4295491584 | bytes 13631488 | tf_op jit(solution)/shard_map/dot_general | solution.py:66
  248.9 1.0 copy-done.3
  249.8 5.6 convolution_multiply_fusion
  255.5 78.3 %reduce-scatter.4.cloned.1.call-done = f32[256,2048]{1,0:T(8,128)} async-done(((f32[1024,2048]{1,0:T(8,128)}), f32[256,2048]{1,0:T(8,128)}) %reduce-scatter.4.cloned.1.call-update) | async-done | bytes 2097168 | tf_op jit(solution)/shard_map/reduce_scatter | solution.py:15
  333.9 0.8 dynamic-slice_subtract_fusion
  334.6 35.3 %reduce-scatter.6.cloned.1.call-done = f32[128,2048]{1,0:T(8,128)} async-done(((f32[256,2048]{1,0:T(8,128)}), f32[128,2048]{1,0:T(8,128)}) %reduce-scatter.6.cloned.1.call-update) | async-done | bytes 1048592 | tf_op jit(solution)/shard_map/reduce_scatter | solution.py:15
  369.9 1.4 reduce_max.9
  371.3 1.6 exponential_reduce_fusion
  372.9 14.4 %all_to_all.5 = f32[16,3,128]{2,1,0:T(4,128)S(1)} all-to-all(f32[16,3,128]{2,1,0:T(4,128)S(1)} %broadcast_in_dim.28), channel_id=1, replica_groups=mesh['psg'=16,'qry_0'=4,'qry_1'=2] {'psg'}, dimensions={0} | all-to-all | bytes 49152 | tf_op jit(solution)/shard_map/all_to_all | solution.py:21
  387.7 0.5 bitcast_subtract_fusion
  388.3 2.4 subtract_convert_fusion
  390.8 87.4 %all-gather.8.cloned.1.call-done = bf16[1024,2048]{1,0:T(8,128)(2,1)} async-done(((bf16[128,2048]{1,0:T(8,128)(2,1)}), bf16[1024,2048]{1,0:T(8,128)(2,1)}) %all-gather.8.cloned.1.call-update) | async-done | bytes 4194320 | tf_op jit(solution)/shard_map/all_gather | solution.py:110
  478.2 5.9 multiply_convert_fusion
  484.1 2.9 copy.19
  487.0 2.8 reshape.74
  489.8 3.3 copy.20
  493.1 35.0 %while.22 = (s32[]{:T(128)}, f32[64,8,256]{2,1,0:T(8,128)S(1)}, bf16[4,512,64,8]{1,3,2,0:T(8,128)(2,1)}, s32[4,512,64]{1,2,0:T(8,128)S(1)}, s32[]{:T(128)}, /*index=5*/s32[]{:T(128)}) while((s32[]{:T(128)}, f32[64,8,256]{2,1,0:T(8,128)S(1)}, bf16[4,512,64,8]{1,3,2,0:T(8,128)(2,1)}, s32[4,512,64]{1,2,0:T(8,128)S(1)}, s32[]{:T(128)}, ...), condition=%wide.region_13.14_spmd.clone, body=%wide.region_12.13_spmd.clone.sunk | while | flops 142868480 | bytes 1966675 | solution.py:132
  493.1 8.7 %fusion.45 = f32[64,8,256]{2,1,0:T(8,128)S(1)} fusion(s32[512,64]{0,1:T(8,128)S(1)} %dynamic-slice_bitcast_fusion.5, f32[64,8,256]{2,1,0:T(8,128)S(1)} %get-tuple-element.191, bf16[4,512,64,8]{1,3,2,0:T(8,128)(2,1)} %get-tuple-element.198, s32[]{:T(128)} %get-tuple-element.190, pred[]{:T(512)S(6)} %compare.3), kind=kOutput, calls=%fused_computation.10.clone.1 | convolution fusion | flops 142868480 | bytes 1704449 | tf_op jit(solution)/shard_map/while/body/eval_jaxpr/pmk,pmd->mdk/dot_general | solution.py:128
  501.9 8.7 %fusion.45 = f32[64,8,256]{2,1,0:T(8,128)S(1)} fusion(s32[512,64]{0,1:T(8,128)S(1)} %dynamic-slice_bitcast_fusion.5, f32[64,8,256]{2,1,0:T(8,128)S(1)} %get-tuple-element.191, bf16[4,512,64,8]{1,3,2,0:T(8,128)(2,1)} %get-tuple-element.198, s32[]{:T(128)} %get-tuple-element.190, pred[]{:T(512)S(6)} %compare.3), kind=kOutput, calls=%fused_computation.10.clone.1 | convolution fusion | flops 142868480 | bytes 1704449 | tf_op jit(solution)/shard_map/while/body/eval_jaxpr/pmk,pmd->mdk/dot_general | solution.py:128
  510.6 8.7 %fusion.45 = f32[64,8,256]{2,1,0:T(8,128)S(1)} fusion(s32[512,64]{0,1:T(8,128)S(1)} %dynamic-slice_bitcast_fusion.5, f32[64,8,256]{2,1,0:T(8,128)S(1)} %get-tuple-element.191, bf16[4,512,64,8]{1,3,2,0:T(8,128)(2,1)} %get-tuple-element.198, s32[]{:T(128)} %get-tuple-element.190, pred[]{:T(512)S(6)} %compare.3), kind=kOutput, calls=%fused_computation.10.clone.1 | convolution fusion | flops 142868480 | bytes 1704449 | tf_op jit(solution)/shard_map/while/body/eval_jaxpr/pmk,pmd->mdk/dot_general | solution.py:128
  519.4 8.7 %fusion.45 = f32[64,8,256]{2,1,0:T(8,128)S(1)} fusion(s32[512,64]{0,1:T(8,128)S(1)} %dynamic-slice_bitcast_fusion.5, f32[64,8,256]{2,1,0:T(8,128)S(1)} %get-tuple-element.191, bf16[4,512,64,8]{1,3,2,0:T(8,128)(2,1)} %get-tuple-element.198, s32[]{:T(128)} %get-tuple-element.190, pred[]{:T(512)S(6)} %compare.3), kind=kOutput, calls=%fused_computation.10.clone.1 | convolution fusion | flops 142868480 | bytes 1704449 | tf_op jit(solution)/shard_map/while/body/eval_jaxpr/pmk,pmd->mdk/dot_general | solution.py:128
  528.1 0.7 convert_element_type.58
  528.9 6.5 convolution_multiply_fusion.1
  535.4 77.4 %all-reduce.4 = bf16[1024,512]{1,0:T(8,128)(2,1)S(1)} all-reduce(f32[1024,512]{1,0:T(8,128)} %convolution_multiply_fusion.1), channel_id=1, replica_groups=mesh['psg'=16,'qry_0'=4,'qry_1'=2] {'psg'}, use_global_device_ids=true, to_apply=%region_9.10 | all-reduce | flops 524288 | bytes 3145728 | tf_op jit(solution)/shard_map/psum | solution.py:112
  612.8 8.9 %convolution_convert_fusion = bf16[1024,4096]{1,0:T(8,128)(2,1)} fusion(bf16[4096,512]{1,0:T(8,128)(2,1)} %all-gather.6.cloned.1.call-done, bf16[1024,512]{1,0:T(8,128)(2,1)S(1)} %all-reduce.4), kind=kOutput, calls=%fused_computation.20 | convolution fusion | flops 4299161600 | bytes 13631488 | tf_op jit(solution)/shard_map/dot_general | solution.py:141
  621.8 2.4 fusion.20
  624.2 44.1 %all-reduce.3.cloned.1.call-done = bf16[64,8,256]{2,1,0:T(8,128)(2,1)} async-done(((bf16[64,8,256]{2,1,0:T(8,128)(2,1)}), bf16[64,8,256]{2,1,0:T(8,128)(2,1)}) %all-reduce.3.cloned.1.call-update) | async-done | bytes 262160 | tf_op jit(solution)/shard_map/psum | solution.py:135
  668.2 1.8 convert_element_type.59
  670.0 170.9 %reduce-scatter.8.cloned.1.call-done = bf16[128,4096]{1,0:T(8,128)(2,1)} async-done(((bf16[1024,4096]{1,0:T(8,128)(2,1)}), bf16[128,4096]{1,0:T(8,128)(2,1)}) %reduce-scatter.8.cloned.1.call-update) | async-done | bytes 1048592 | tf_op jit(solution)/shard_map/reduce_scatter | solution.py:144
  840.9 1.8 fusion.13
  842.7 2.9 fusion.18
  (63 shorter events, 1.6 us)
Async XLA Ops:
  7.2 173.7 %all-gather.4.cloned.1.call-start = ((), (), s32[]{:S(2)}) async-start(), calls=%async_computation.4 | async-start | bytes 9437184 | tf_op jit(solution)/shard_map/all_gather | solution.py:60
  7.9 231.9 %all-gather.6.cloned.1.call-start = ((), (), s32[]{:S(2)}) async-start(), calls=%async_computation.5 | async-start | bytes 4456448 | tf_op jit(solution)/shard_map/all_gather | solution.py:65
  8.6 325.1 %reduce-scatter.4.cloned.1.call-start = ((), (), s32[]{:S(2)}) async-start(), calls=%async_computation.6 | async-start | bytes 10485760 | tf_op jit(solution)/shard_map/reduce_scatter | solution.py:15
  42.9 143.1 %copy-start.1 = (f32[4096]{0:T(1024)S(1)}, f32[4096]{0:T(1024)}, u32[]{:S(2)}) copy-start(f32[4096]{0:T(1024)} %param.11) | copy-start | bytes 49156
  196.3 53.5 %copy-start.2 = (bf16[4,512,512]{2,1,0:T(8,128)(2,1)S(1)}, bf16[4,512,512]{2,1,0:T(8,128)(2,1)}, u32[]{:S(2)}) copy-start(bf16[4,512,512]{2,1,0:T(8,128)(2,1)} %get-tuple-element.48) | copy-start | bytes 6291460
  248.9 1.0 copy-start.3
  255.5 222.7 %copy-start.4 = (bf16[1024,512]{1,0:T(8,128)(2,1)S(1)}, bf16[1024,512]{1,0:T(8,128)(2,1)}, u32[]{:S(2)}) copy-start(bf16[1024,512]{1,0:T(8,128)(2,1)} %copy-done.3) | copy-start | bytes 3145732
  255.5 114.4 %reduce-scatter.6.cloned.1.call-start = ((), (), s32[]{:S(2)}) async-start(), calls=%async_computation.7 | async-start | bytes 3145728 | tf_op jit(solution)/shard_map/reduce_scatter | solution.py:15
  333.8 144.4 %all-gather.8.cloned.1.call-start = ((), (), s32[]{:S(2)}) async-start(), calls=%async_computation.8 | async-start | bytes 4718592 | tf_op jit(solution)/shard_map/all_gather | solution.py:110
  390.7 277.5 %all-reduce.3.cloned.1.call-start = ((), (), s32[]{:S(2)}) async-start(), calls=%async_computation.10 | async-start | bytes 524288 | tf_op jit(solution)/shard_map/psum | solution.py:135
  528.9 312.1 %reduce-scatter.8.cloned.1.call-start = ((), (), s32[]{:S(2)}) async-start(), calls=%async_computation.9 | async-start | bytes 9437184 | tf_op jit(solution)/shard_map/reduce_scatter | solution.py:144
  621.8 219.2 %copy-start = (bf16[128,4096]{1,0:T(8,128)(2,1)S(1)}, bf16[128,4096]{1,0:T(8,128)(2,1)}, u32[]{:S(2)}) copy-start(bf16[128,4096]{1,0:T(8,128)(2,1)} %param.10) | copy-start | bytes 3145732
Sparse Core Ops, SparseCore 0:
  9.6 171.2 all-gather.3
  183.4 56.3 all-gather.5
  255.6 78.1 reduce-scatter.3
  336.0 33.8 reduce-scatter.5
  390.9 87.2 all-gather.7
  529.0 139.1 all-reduce.2
  670.6 170.2 reduce-scatter.7
where the time goes:
time: 854 us; the launch traced here: 852 us
  waiting for transfers between devices  599 us (70%)
  matrix products  102 us (12%)
  blocking collectives  91.8 us (11%)
  other arithmetic  29.4 us (3%)
  local copies, waits for them, and re-layouts  15.8 us (2%)
  between operations  14.3 us (2%)
    reduce_scatter x1, waiting for transfers between devices, per_device(): lax.psum_scatter(norm_part.astype(jnp.bfloat16), QRY, scatter_dimension=0...  171 us
    all_gather x1, waiting for transfers between devices, per_device(): gathered = lax.all_gather(hidden, QRY, axis=0, tiled=True)  138 us
    reduce_scatter x2, waiting for transfers between devices, summed_rows(): nearer = lax.psum_scatter(x, axes[0], scatter_dimension=dim, tiled=True)  114 us
    all_gather x1, waiting for transfers between devices, per_device(): all_grad = lax.all_gather(score_grad, QRY, axis=0, tiled=True)  87.4 us
    psum x1, blocking collectives, per_device(): query_grad = lax.psum(query_part, 'psg').astype(jnp.bfloat16)  77.4 us
    psum x1, waiting for transfers between devices, per_device(): lax.psum(book_part.astype(jnp.bfloat16), 'psg').astype(jnp.float32)  44.1 us
    all_gather x1, waiting for transfers between devices, per_device(): whole_weight = lax.all_gather(proj_weight, 'psg', axis=0, tiled=True)  43.5 us
    dot_general x4, matrix products, add_book(): jnp.einsum('pmk,pmd->mdk', hot_table, grad_block, preferred_element_type=...  34.9 us
  transfers between devices with their start and end apart: 7, of which 7 were waited for; matrix products, arithmetic and copies ran while one was open for 8% of the time, Pallas kernels for 0%

commit v1 on v0

--- a/solution.py
+++ b/solution.py
@@ -3,6 +3,7 @@
 from jax import lax
 from jax.sharding import Mesh
 from jax.sharding import PartitionSpec as P
+from jax.lax import all_to_all, axis_size
 
 QRY = ("qry_0", "qry_1")
 score_scale = 0.0625
@@ -107,7 +108,10 @@
     score_grad = (
         jnp.exp(scores - row_max[:, None]) / row_total[:, None] - target.astype(jnp.float32)
     ).astype(jnp.bfloat16)
-    all_grad = lax.all_gather(score_grad, QRY, axis=0, tiled=True)
+    rings_put = lambda block_in: jnp.concatenate(
+        all_to_all(jnp.stack(axis_size(QRY) * [block_in], 0), QRY, 0, 0), axis=0
+    )
+    all_grad = rings_put(score_grad)
     query_part = jnp.dot(all_grad, passages, preferred_element_type=jnp.float32) * score_scale
     query_grad = lax.psum(query_part, "psg").astype(jnp.bfloat16)
     passage_grad = (

time: 854 us -> 824 us (0.965)
  waiting for transfers between devices: 599 us -> 566 us
    all_gather x1 -> x0, waiting for transfers between devices: 87.4 us -> none  [per_device(): all_grad = lax.all_gather(score_grad, QRY, axis=0, tiled=True)]
    all_to_all x0 -> x1, waiting for transfers between devices: none -> 49.1 us  [per_device(): all_to_all(jnp.stack(axis_size(QRY) * [block_in], 0), QRY, 0, 0)]
where the time goes in v1:
time: 824 us; the launch traced here: 822 us
  waiting for transfers between devices  566 us (69%)
  matrix products  102 us (12%)
  blocking collectives  88.1 us (11%)
  other arithmetic  28.6 us (3%)
  local copies, waits for them, and re-layouts  18.3 us (2%)
  between operations  14.3 us (2%)
    reduce_scatter x1, waiting for transfers between devices, per_device(): lax.psum_scatter(norm_part.astype(jnp.bfloat16), QRY, scatter_dimension=0...  171 us
    all_gather x1, waiting for transfers between devices, per_device(): gathered = lax.all_gather(hidden, QRY, axis=0, tiled=True)  138 us
    reduce_scatter x2, waiting for transfers between devices, summed_rows(): nearer = lax.psum_scatter(x, axes[0], scatter_dimension=dim, tiled=True)  114 us
    psum x1, blocking collectives, per_device(): query_grad = lax.psum(query_part, 'psg').astype(jnp.bfloat16)  73.7 us
    psum x1, waiting for transfers between devices, per_device(): lax.psum(book_part.astype(jnp.bfloat16), 'psg').astype(jnp.float32)  50 us
    all_to_all x1, waiting for transfers between devices, per_device(): all_to_all(jnp.stack(axis_size(QRY) * [block_in], 0), QRY, 0, 0)  49.1 us
    all_gather x1, waiting for transfers between devices, per_device(): whole_weight = lax.all_gather(proj_weight, 'psg', axis=0, tiled=True)  43.5 us
    dot_general x4, matrix products, add_book(): jnp.einsum('pmk,pmd->mdk', hot_table, grad_block, preferred_element_type=...  34.9 us
  transfers between devices with their start and end apart: 7, of which 7 were waited for; matrix products, arithmetic and copies ran while one was open for 8% of the time, Pallas kernels for 0%

profile of v1, /device:TPU:1, one launch (start us, length us, event | category | flops | bytes accessed | tf_op | source)
XLA Modules:
  0.0 822.4 jit_solution(16388595712604016938)
XLA Ops:
  7.2 0.7 all-gather.3.cloned.1.call-update
  7.9 0.7 all-gather.5.cloned.1.call-update
  8.7 1.1 copy.27
  9.8 33.1 %while.21 = (s32[]{:T(128)}, bf16[4,512,512]{2,1,0:T(8,128)(2,1)}, s32[4,512,64]{1,2,0:T(8,128)S(1)}, bf16[64,8,256]{2,1,0:T(8,128)(2,1)}, s32[]{:T(128)}) while((s32[]{:T(128)}, bf16[4,512,512]{2,1,0:T(8,128)(2,1)}, s32[4,512,64]{1,2,0:T(8,128)S(1)}, bf16[64,8,256]{2,1,0:T(8,128)(2,1)}, s32[]{:T(128)}) %tuple.72), condition=%wide.region_2.3_spmd, body=%wide.region_1.2_spmd.sunk | while | flops 142868480 | bytes 3277377 | solution.py:82
  9.8 7.2 fusion.43
  17.2 0.8 constant_dynamic-update-slice_fusion.2
  18.1 7.2 fusion.43
  25.5 0.8 constant_dynamic-update-slice_fusion.2
  26.4 7.2 fusion.43
  33.8 0.9 constant_dynamic-update-slice_fusion.2
  34.6 7.2 fusion.43
  42.1 0.8 constant_dynamic-update-slice_fusion.2
  42.9 138.0 %all-gather.3.cloned.1.call-done = bf16[1024,4096]{1,0:T(8,128)(2,1)} async-done(((bf16[128,4096]{1,0:T(8,128)(2,1)}), bf16[1024,4096]{1,0:T(8,128)(2,1)}) %all-gather.3.cloned.1.call-update) | async-done | bytes 8388624 | tf_op jit(solution)/shard_map/all_gather | solution.py:61
  180.9 5.1 fusion.10
  186.0 10.3 %fusion.12 = bf16[1024,4096]{1,0:T(8,128)(2,1)} fusion(bf16[1024,4096]{1,0:T(8,128)(2,1)} %all-gather.3.cloned.1.call-done, f32[4096]{0:T(1024)S(1)} %copy-done.1, f32[1024]{0:T(1024)S(1)} %add_rsqrt_fusion), kind=kLoop, calls=%fused_computation.19 | loop fusion | flops 16777216 | bytes 16797696 | tf_op jit(solution)/shard_map/convert_element_type | solution.py:64
  196.3 43.5 %all-gather.5.cloned.1.call-done = bf16[4096,512]{1,0:T(8,128)(2,1)} async-done(((bf16[256,512]{1,0:T(8,128)(2,1)}), bf16[4096,512]{1,0:T(8,128)(2,1)}) %all-gather.5.cloned.1.call-update) | async-done | bytes 4194320 | tf_op jit(solution)/shard_map/all_gather | solution.py:66
  239.8 9.1 %convolution_convert_fusion.1 = bf16[1024,512]{1,0:T(8,128)(2,1)S(1)} fusion(bf16[1024,4096]{1,0:T(8,128)(2,1)} %fusion.12, bf16[4096,512]{1,0:T(8,128)(2,1)} %all-gather.5.cloned.1.call-done), kind=kOutput, calls=%fused_computation.35 | convolution fusion | flops 4295491584 | bytes 13631488 | tf_op jit(solution)/shard_map/dot_general | solution.py:67
  248.9 1.0 copy-done.3
  249.8 5.6 convolution_multiply_fusion
  255.5 78.3 %reduce-scatter.4.cloned.1.call-done = f32[256,2048]{1,0:T(8,128)} async-done(((f32[1024,2048]{1,0:T(8,128)}), f32[256,2048]{1,0:T(8,128)}) %reduce-scatter.4.cloned.1.call-update) | async-done | bytes 2097168 | tf_op jit(solution)/shard_map/reduce_scatter | solution.py:16
  333.8 0.8 dynamic-slice_subtract_fusion
  334.6 35.3 %reduce-scatter.6.cloned.1.call-done = f32[128,2048]{1,0:T(8,128)} async-done(((f32[256,2048]{1,0:T(8,128)}), f32[128,2048]{1,0:T(8,128)}) %reduce-scatter.6.cloned.1.call-update) | async-done | bytes 1048592 | tf_op jit(solution)/shard_map/reduce_scatter | solution.py:16
  369.9 1.4 reduce_max.9
  371.2 1.6 exponential_reduce_fusion
  372.9 14.4 %all_to_all.10 = f32[16,3,128]{2,1,0:T(4,128)S(1)} all-to-all(f32[16,3,128]{2,1,0:T(4,128)S(1)} %broadcast_in_dim.28), channel_id=1, replica_groups=mesh['psg'=16,'qry_0'=4,'qry_1'=2] {'psg'}, dimensions={0} | all-to-all | bytes 49152 | tf_op jit(solution)/shard_map/all_to_all | solution.py:22
  388.2 1.6 subtract_convert_fusion
  389.9 2.5 stack.2
  392.4 4.6 all-to-all-start.1
  397.0 49.1 %all-to-all-done.1 = bf16[8,128,2048]{2,1,0:T(8,128)(2,1)} async-done(((bf16[8,128,2048]{2,1,0:T(8,128)(2,1)}), bf16[8,128,2048]{2,1,0:T(8,128)(2,1)}, u32[]{:S(2)}, u32[]{:S(2)}) %all-to-all-start.1) | async-done | bytes 4194336 | tf_op jit(solution)/shard_map/all_to_all | solution.py:112
  446.1 6.2 multiply_convert_fusion
  452.3 5.9 convolution_multiply_fusion.1
  458.2 2.9 copy.19
  461.1 2.8 reshape.80
  463.9 3.4 copy.20
  467.3 35.0 %while.22 = (s32[]{:T(128)}, f32[64,8,256]{2,1,0:T(8,128)S(1)}, bf16[4,512,64,8]{1,3,2,0:T(8,128)(2,1)}, s32[4,512,64]{1,2,0:T(8,128)S(1)}, s32[]{:T(128)}, /*index=5*/s32[]{:T(128)}) while((s32[]{:T(128)}, f32[64,8,256]{2,1,0:T(8,128)S(1)}, bf16[4,512,64,8]{1,3,2,0:T(8,128)(2,1)}, s32[4,512,64]{1,2,0:T(8,128)S(1)}, s32[]{:T(128)}, ...), condition=%wide.region_13.14_spmd.clone, body=%wide.region_12.13_spmd.clone.sunk | while | flops 142868480 | bytes 1966675 | solution.py:136
  467.3 8.7 %fusion.45 = f32[64,8,256]{2,1,0:T(8,128)S(1)} fusion(s32[512,64]{0,1:T(8,128)S(1)} %dynamic-slice_bitcast_fusion.5, f32[64,8,256]{2,1,0:T(8,128)S(1)} %get-tuple-element.191, bf16[4,512,64,8]{1,3,2,0:T(8,128)(2,1)} %get-tuple-element.198, s32[]{:T(128)} %get-tuple-element.190, pred[]{:T(512)S(6)} %compare.3), kind=kOutput, calls=%fused_computation.10.clone.1 | convolution fusion | flops 142868480 | bytes 1704449 | tf_op jit(solution)/shard_map/while/body/eval_jaxpr/pmk,pmd->mdk/dot_general | solution.py:132
  476.1 8.7 %fusion.45 = f32[64,8,256]{2,1,0:T(8,128)S(1)} fusion(s32[512,64]{0,1:T(8,128)S(1)} %dynamic-slice_bitcast_fusion.5, f32[64,8,256]{2,1,0:T(8,128)S(1)} %get-tuple-element.191, bf16[4,512,64,8]{1,3,2,0:T(8,128)(2,1)} %get-tuple-element.198, s32[]{:T(128)} %get-tuple-element.190, pred[]{:T(512)S(6)} %compare.3), kind=kOutput, calls=%fused_computation.10.clone.1 | convolution fusion | flops 142868480 | bytes 1704449 | tf_op jit(solution)/shard_map/while/body/eval_jaxpr/pmk,pmd->mdk/dot_general | solution.py:132
  484.9 8.7 %fusion.45 = f32[64,8,256]{2,1,0:T(8,128)S(1)} fusion(s32[512,64]{0,1:T(8,128)S(1)} %dynamic-slice_bitcast_fusion.5, f32[64,8,256]{2,1,0:T(8,128)S(1)} %get-tuple-element.191, bf16[4,512,64,8]{1,3,2,0:T(8,128)(2,1)} %get-tuple-element.198, s32[]{:T(128)} %get-tuple-element.190, pred[]{:T(512)S(6)} %compare.3), kind=kOutput, calls=%fused_computation.10.clone.1 | convolution fusion | flops 142868480 | bytes 1704449 | tf_op jit(solution)/shard_map/while/body/eval_jaxpr/pmk,pmd->mdk/dot_general | solution.py:132
  493.6 8.7 %fusion.45 = f32[64,8,256]{2,1,0:T(8,128)S(1)} fusion(s32[512,64]{0,1:T(8,128)S(1)} %dynamic-slice_bitcast_fusion.5, f32[64,8,256]{2,1,0:T(8,128)S(1)} %get-tuple-element.191, bf16[4,512,64,8]{1,3,2,0:T(8,128)(2,1)} %get-tuple-element.198, s32[]{:T(128)} %get-tuple-element.190, pred[]{:T(512)S(6)} %compare.3), kind=kOutput, calls=%fused_computation.10.clone.1 | convolution fusion | flops 142868480 | bytes 1704449 | tf_op jit(solution)/shard_map/while/body/eval_jaxpr/pmk,pmd->mdk/dot_general | solution.py:132
  502.4 0.7 convert_element_type.58
  503.2 73.7 %all-reduce.4 = bf16[1024,512]{1,0:T(8,128)(2,1)S(1)} all-reduce(f32[1024,512]{1,0:T(8,128)} %convolution_multiply_fusion.1), channel_id=1, replica_groups=mesh['psg'=16,'qry_0'=4,'qry_1'=2] {'psg'}, use_global_device_ids=true, to_apply=%region_9.10 | all-reduce | flops 524288 | bytes 3145728 | tf_op jit(solution)/shard_map/psum | solution.py:116
  576.9 8.9 %convolution_convert_fusion = bf16[1024,4096]{1,0:T(8,128)(2,1)} fusion(bf16[4096,512]{1,0:T(8,128)(2,1)} %all-gather.5.cloned.1.call-done, bf16[1024,512]{1,0:T(8,128)(2,1)S(1)} %all-reduce.4), kind=kOutput, calls=%fused_computation.20 | convolution fusion | flops 4299161600 | bytes 13631488 | tf_op jit(solution)/shard_map/dot_general | solution.py:145
  585.9 2.4 fusion.20
  588.2 50.0 %all-reduce.3.cloned.1.call-done = bf16[64,8,256]{2,1,0:T(8,128)(2,1)} async-done(((bf16[64,8,256]{2,1,0:T(8,128)(2,1)}), bf16[64,8,256]{2,1,0:T(8,128)(2,1)}) %all-reduce.3.cloned.1.call-update) | async-done | bytes 262160 | tf_op jit(solution)/shard_map/psum | solution.py:139
  638.3 1.8 convert_element_type.59
  640.1 170.8 %reduce-scatter.8.cloned.1.call-done = bf16[128,4096]{1,0:T(8,128)(2,1)} async-done(((bf16[1024,4096]{1,0:T(8,128)(2,1)}), bf16[128,4096]{1,0:T(8,128)(2,1)}) %reduce-scatter.8.cloned.1.call-update) | async-done | bytes 1048592 | tf_op jit(solution)/shard_map/reduce_scatter | solution.py:148
  810.9 1.8 fusion.13
  812.7 2.9 fusion.18
  (61 shorter events, 2.3 us)
Async XLA Ops:
  7.2 173.7 %all-gather.3.cloned.1.call-start = ((), (), s32[]{:S(2)}) async-start(), calls=%async_computation.5 | async-start | bytes 9437184 | tf_op jit(solution)/shard_map/all_gather | solution.py:61
  7.9 231.9 %all-gather.5.cloned.1.call-start = ((), (), s32[]{:S(2)}) async-start(), calls=%async_computation.6 | async-start | bytes 4456448 | tf_op jit(solution)/shard_map/all_gather | solution.py:66
  8.6 325.1 %reduce-scatter.4.cloned.1.call-start = ((), (), s32[]{:S(2)}) async-start(), calls=%async_computation.7 | async-start | bytes 10485760 | tf_op jit(solution)/shard_map/reduce_scatter | solution.py:16
  42.9 143.1 %copy-start.1 = (f32[4096]{0:T(1024)S(1)}, f32[4096]{0:T(1024)}, u32[]{:S(2)}) copy-start(f32[4096]{0:T(1024)} %param.11) | copy-start | bytes 49156
  196.3 53.5 %copy-start.2 = (bf16[4,512,512]{2,1,0:T(8,128)(2,1)S(1)}, bf16[4,512,512]{2,1,0:T(8,128)(2,1)}, u32[]{:S(2)}) copy-start(bf16[4,512,512]{2,1,0:T(8,128)(2,1)} %get-tuple-element.48) | copy-start | bytes 6291460
  248.9 1.0 copy-start.3
  255.4 114.4 %reduce-scatter.6.cloned.1.call-start = ((), (), s32[]{:S(2)}) async-start(), calls=%async_computation.8 | async-start | bytes 3145728 | tf_op jit(solution)/shard_map/reduce_scatter | solution.py:16
  392.4 53.8 %all-to-all-start.1 = ((bf16[8,128,2048]{2,1,0:T(8,128)(2,1)}), bf16[8,128,2048]{2,1,0:T(8,128)(2,1)}, u32[]{:S(2)}, u32[]{:S(2)}) async-start(bf16[8,128,2048]{2,1,0:T(8,128)(2,1)} %stack.2), calls=%async_computation.3 | async-start | bytes 8388608 | tf_op jit(solution)/shard_map/all_to_all | solution.py:112
  397.0 241.3 %all-reduce.3.cloned.1.call-start = ((), (), s32[]{:S(2)}) async-start(), calls=%async_computation.10 | async-start | bytes 524288 | tf_op jit(solution)/shard_map/psum | solution.py:139
  503.1 307.7 %reduce-scatter.8.cloned.1.call-start = ((), (), s32[]{:S(2)}) async-start(), calls=%async_computation.9 | async-start | bytes 9437184 | tf_op jit(solution)/shard_map/reduce_scatter | solution.py:148
  585.8 225.0 %copy-start = (bf16[128,4096]{1,0:T(8,128)(2,1)S(1)}, bf16[128,4096]{1,0:T(8,128)(2,1)}, u32[]{:S(2)}) copy-start(bf16[128,4096]{1,0:T(8,128)(2,1)} %param.10) | copy-start | bytes 3145732
Sparse Core Ops, SparseCore 0:
  9.6 171.2 all-gather.2
  183.4 56.3 all-gather.4
  255.6 78.1 reduce-scatter.3
  336.0 33.8 reduce-scatter.5
  503.2 135.0 all-reduce.2
  640.5 170.2 reduce-scatter.7
